TPU v7x, 32 devices: a whole 2x2x4 slice. The times are simulated.
32 devices in a mesh: rows: 16 (over z, x, core), chan: 2 (over y).
Axes of the slice: x: 2, y: 2, z: 4, core: 2. Of those that a mesh axis runs over, the one named last changes fastest.
Arguments:
- pixels: float32 [1024, 16384], P(('chan', 'rows')), parts along dimension 0, may hold values from -6 to 6
- row_taps: float32 [32768], P(('chan', 'rows')), parts along dimension 0, may hold values from -0.046875 to 0.046875
- column_taps: float32 [1024], P(('chan', 'rows')), parts along dimension 0, may hold values from -0.25 to 0.25
- stencil: float32 [6, 3], P('chan'), parts along dimension 0, may hold values from -3 to 3
Outputs:
- filtered: float32 [1024, 16384], P(('chan', 'rows')), parts along dimension 0
There are 2 independent parts, one for each index of `chan`. A program takes and returns all parts, laid end to end along the dimension named above; each array names one. Nothing has to cross between parts.
All inputs are finite; a program needn't handle non-finite values.
Results may differ from a plain program's by a relative error of at most 0.0003.
Values sent between devices are 32-bit elements; how exact they have to be, the bound alone decides.
A program may use at most 128 MiB of HBM per device.

v0:
```python
import math

import jax
import jax.numpy as jnp
from jax import lax
from jax.sharding import PartitionSpec as P

dft_precision = lax.Precision.HIGH
row_forms = ("kj,rjm->rkm", "rkm,ml->rkl")
column_forms = ("kj,jmc->kmc", "kmc,ml->klc")


def padded_2(cells, sides, width):
    for axis, dim in sides:
        count = lax.axis_size(axis)
        head = lax.slice_in_dim(cells, 0, width, axis=dim)
        tail = lax.slice_in_dim(cells, cells.shape[dim] - width, cells.shape[dim], axis=dim)
        cells = jnp.concatenate(
            [
                lax.ppermute(tail, axis, [(i, (i + 1) % count) for i in range(count)]),
                cells,
                lax.ppermute(head, axis, [((i + 1) % count, i) for i in range(count)]),
            ],
            axis=dim,
        )
    return cells


def split_length(length):
    factor = int(math.isqrt(length))
    while length % factor:
        factor -= 1
    return (length // factor, factor)


def dft_tables(length):
    positions = jnp.arange(length, dtype=jnp.int32)
    product = positions[:, None] * positions[None, :] % length
    angles = product.astype(jnp.float32) * (2.0 * math.pi / length)
    return (jnp.cos(angles), -jnp.sin(angles))


def prepare(length, twist_shape):
    outer_len, inner_len = split_length(length)
    cos_outer, sin_outer = dft_tables(outer_len)
    cos_inner, sin_inner = dft_tables(inner_len)
    outer_pos = jnp.arange(outer_len, dtype=jnp.int32)
    inner_pos = jnp.arange(inner_len, dtype=jnp.int32)
    product = outer_pos[:, None] * inner_pos[None, :] % length
    angles = product.astype(jnp.float32) * (2.0 * math.pi / length)
    twist_real = jnp.cos(angles).reshape(twist_shape)
    twist_imag = (-jnp.sin(angles)).reshape(twist_shape)
    return (
        outer_len,
        inner_len,
        cos_outer,
        sin_outer,
        cos_inner,
        sin_inner,
        twist_real,
        twist_imag,
    )


def contract(form, left, right):
    return jnp.einsum(
        form, left, right, precision=dft_precision, preferred_element_type=jnp.float32
    )


def forward(values, tables, forms):
    outer_len, inner_len, cos_outer, sin_outer, cos_inner, sin_inner, twist_real, twist_imag = (
        tables
    )
    first_real = contract(forms[0], cos_outer, values)
    first_imag = contract(forms[0], sin_outer, values)
    turned_real = first_real * twist_real - first_imag * twist_imag
    turned_imag = first_real * twist_imag + first_imag * twist_real
    out_real = contract(forms[1], turned_real, cos_inner) - contract(
        forms[1], turned_imag, sin_inner
    )
    out_imag = contract(forms[1], turned_real, sin_inner) + contract(
        forms[1], turned_imag, cos_inner
    )
    return (out_real, out_imag)


def inverse(spec_real, spec_imag, tables, forms):
    outer_len, inner_len, cos_outer, sin_outer, cos_inner, sin_inner, twist_real, twist_imag = (
        tables
    )
    back_real = contract(forms[1], spec_real, cos_inner) + contract(forms[1], spec_imag, sin_inner)
    back_imag = contract(forms[1], spec_imag, cos_inner) - contract(forms[1], spec_real, sin_inner)
    turned_real = back_real * twist_real + back_imag * twist_imag
    turned_imag = back_imag * twist_real - back_real * twist_imag
    result = contract(forms[0], cos_outer, turned_real) + contract(forms[0], sin_outer, turned_imag)
    return result / float(outer_len * inner_len)


def convolve(values, filter_spec, tables, forms):
    spec_real, spec_imag = forward(values, tables, forms)
    filter_real, filter_imag = filter_spec
    prod_real = spec_real * filter_real - spec_imag * filter_imag
    prod_imag = spec_real * filter_imag + spec_imag * filter_real
    return inverse(prod_real, prod_imag, tables, forms)


def body(pixels, row_taps, column_taps, stencil):
    rows_dev, row_length = pixels.shape
    devices_rows = lax.axis_size("rows")
    whole_row, whole_column = (
        lax.all_gather(row_taps, "rows", axis=0, tiled=True),
        lax.all_gather(column_taps, "rows", axis=0, tiled=True),
    )
    column_length = whole_column.shape[0]
    row_tables = prepare(row_length, (1, split_length(row_length)[0], split_length(row_length)[1]))
    column_tables = prepare(
        column_length, (split_length(column_length)[0], split_length(column_length)[1], 1)
    )
    row_filter = forward(whole_row.reshape(1, row_tables[0], row_tables[1]), row_tables, row_forms)
    column_filter = forward(
        whole_column.reshape(column_tables[0], column_tables[1], 1), column_tables, column_forms
    )
    cols_dev = row_length // devices_rows
    lane_width = min(128, cols_dev)
    groups = cols_dev // lane_width
    padded = padded_2(pixels, (("rows", 0),), 1)
    shaped = pixels.reshape(pixels.shape[0], row_tables[0], row_tables[1])
    blocks = (
        convolve(shaped, row_filter, row_tables, row_forms)
        .reshape(pixels.shape)
        .reshape(rows_dev, groups, devices_rows * lane_width)
    )
    moved = lax.all_to_all(blocks, "rows", split_axis=2, concat_axis=0, tiled=True)
    shaped = moved.reshape(column_tables[0], column_tables[1], -1)
    result = lax.all_to_all(
        convolve(shaped, column_filter, column_tables, column_forms).reshape(moved.shape),
        "rows",
        split_axis=0,
        concat_axis=2,
        tiled=True,
    )
    convolved = result.reshape(rows_dev, row_length)
    filtered = convolved
    for offset_row in range(3):
        row_band = padded[offset_row : offset_row + rows_dev]
        for offset_col in range(3):
            filtered = filtered + stencil[offset_row, offset_col] * jnp.roll(
                row_band, 1 - offset_col, axis=1
            )
    return filtered


def solution(mesh):
    in_specs = (
        P(("chan", "rows"), None),
        P(("chan", "rows")),
        P(("chan", "rows")),
        P("chan", None),
    )
    out_specs = P(("chan", "rows"), None)
    return jax.shard_map(body, mesh=mesh, in_specs=in_specs, out_specs=out_specs, check_vma=False)
```

profile of v0, /device:TPU:0, one launch (start us, length us, event | category | flops | bytes accessed | tf_op | source)
XLA Modules:
  0.0 284.7 jit_solution(11829986946056590800)
XLA Ops:
  0.0 0.3 sine_negate_fusion.1
  0.3 2.0 copy.92
  2.2 1.3 fusion.108
  3.6 1.3 fusion.115
  4.9 1.4 fusion.26
  6.3 1.3 fusion.24
  7.7 23.6 %all_gather.6 = f32[16384]{0:T(1024)S(1)} all-gather(f32[1024]{0:T(1024)S(1)} %copy-done.4), channel_id=1, replica_groups=mesh['rows'=16,'chan'=2] {'rows'}, dimensions={0}, use_global_device_ids=true | all-gather | bytes 69632 | tf_op jit(solution)/shard_map/all_gather | solution.py:112
  31.3 0.4 convolution_bitcast_fusion
  31.7 0.4 convolution_bitcast_fusion.1
  32.1 0.7 fusion.97
  32.8 0.7 fusion.99
  33.5 1.4 fusion.60
  34.9 1.4 fusion.63
  36.3 0.7 convolution_add_fusion.1
  36.9 0.7 convolution_subtract_fusion.1
  37.6 1.3 fusion.87
  38.9 1.3 fusion.86
  40.3 1.4 convolution_subtract_fusion
  41.7 1.4 convolution_add_fusion
  43.0 12.9 %fusion.32 = f32[32,128,128]{2,1,0:T(8,128)S(1)} fusion(f32[32,128,128]{2,1,0:T(8,128)S(1)} %convolution_add_fusion, f32[32,128,128]{2,1,0:T(8,128)S(1)} %convolution_subtract_fusion, f32[128,128]{1,0:T(8,128)S(1)} %get-tuple-element.30, f32[128,128]{1,0:T(8,128)S(1)} %get-tuple-element.31), kind=kOutput, calls=%fused_computation.58 | convolution fusion | flops 404471808 | bytes 6422528 | tf_op jit(solution)/shard_map/kj,rjm->rkm/dot_general | solution.py:66
  56.0 3.4 %multiply_bitcast_fusion = f32[32,128,128]{1,2,0:T(8,128)} fusion(f32[32,128,128]{2,1,0:T(8,128)S(1)} %fusion.32, f32[32,128,128]{2,1,0:T(8,128)S(1)} %convolution_subtract_fusion, f32[32,128,128]{2,1,0:T(8,128)S(1)} %convolution_add_fusion, f32[128,128]{1,0:T(8,128)S(1)} %get-tuple-element.30, f32[128,128]{1,0:T(8,128)S(1)} %get-tuple-element.31), kind=kOutput, calls=%fused_computation.57 | convolution fusion | flops 405504000 | bytes 8519680 | tf_op jit(solution)/shard_map/kj,rjm->rkm/dot_general | solution.py:66
  59.4 2.9 %copy.73 = f32[32,128,128]{2,1,0:T(8,128)} copy(f32[32,128,128]{1,2,0:T(8,128)} %multiply_bitcast_fusion) | data formatting | bytes 4194304 | tf_op jit(solution)/shard_map/div | solution.py:97
  62.3 1.7 reshape_reshape.3
  64.0 4.9 %copy.74 = f32[32,8,2048]{0,1,2:T(8,128)} copy(f32[32,8,2048]{2,1,0:T(8,128)S(1)} %reshape_reshape.3) | data formatting | bytes 4194304 | tf_op jit(solution)/shard_map/reshape;reshape | solution.py:132
  68.9 8.6 %reshape.203 = f32[16,1,32768]{2,1,0:T(1,128)} reshape(f32[2048,8,32]{2,1,0:T(8,128)} %bitcast.190) | data formatting | bytes 4194304
  77.4 4.6 %all-to-all-start = ((f32[16,1,32768]{2,1,0:T(1,128)}), f32[16,1,32768]{2,1,0:T(1,128)}, u32[]{:S(2)}, u32[]{:S(2)}) async-start(f32[16,1,32768]{2,1,0:T(1,128)} %reshape.203), calls=%async_computation | async-start | bytes 4194304 | tf_op jit(solution)/shard_map/all_to_all | solution.py:134
  82.1 0.3 collective-permute-start
  82.4 4.2 %collective-permute-start.1 = (f32[1,16384]{1,0:T(1,128)S(1)}, f32[1,16384]{1,0:T(1,128)S(1)}, u32[]{:S(2)}, u32[]{:S(2)}) collective-permute-start(f32[1,16384]{1,0:T(1,128)S(1)} %get-tuple-element.19), channel_id=1, source_target_pairs={{2,0},{4,2},{6,4},{8,6},{10,8},{12,10},{14,12},{16,14},{18,16},{20... | collective-permute-start | bytes 196616 | tf_op jit(solution)/shard_map/ppermute | solution.py:22
  86.6 0.6 dynamic-slice
  87.9 0.2 dynamic-update-slice
  88.1 56.8 %all-reduce = f32[512]{0:T(512)S(1)} all-reduce(f32[512]{0:T(512)S(1)} %dynamic-update-slice), channel_id=1, replica_groups=mesh['rows'=16,'chan'=2] {'rows'}, use_global_device_ids=true, to_apply=%add | all-reduce | flops 512 | bytes 4096
  145.2 0.2 fusion.173
  145.4 0.2 fusion.184
  145.7 0.2 fusion.187
  145.9 1.5 constant_dynamic-update-slice_fusion
  147.8 0.2 fusion.68
  148.0 0.7 fusion.361
  148.8 2.0 dynamic-update-slice.2
  150.8 5.3 %fusion.356 = (f32[32,16383]{1,0:T(8,128)}, f32[32,16383]{1,0:T(8,128)}) fusion(f32[33,16384]{1,0:T(8,128)} %dynamic-update-slice.2), kind=kLoop, calls=%fused_computation.386 | loop fusion | bytes 8388096 | tf_op jit(solution)/shard_map/jit(_roll_static)/slice | solution.py:148
  156.1 0.5 broadcast.381
  156.6 8.6 %reduce = f32[16,32768]{1,0:T(8,128)} reduce(f32[16,1,32768]{2,1,0:T(1,128)} %all-to-all-done, f32[]{:T(128)} %broadcast.381), dimensions={1}, to_apply=%all_to_all.22.reduce_sub_computation | reduce | bytes 4194308 | tf_op jit(solution)/shard_map/all_to_all | solution.py:134
  165.2 6.0 %reshape.204 = f32[2048,8,32]{2,1,0:T(8,128)} reshape(f32[16,32768]{1,0:T(8,128)} %reduce) | data formatting | bytes 4194304
  171.2 6.2 %copy.75 = f32[32,8,16,128]{3,1,0,2:T(8,128)} copy(f32[32,8,16,128]{0,1,3,2:T(8,128)} %bitcast.191) | data formatting | bytes 4194304 | tf_op jit(solution)/shard_map/all_to_all | solution.py:134
  177.4 3.1 %reshape.188 = f32[32,16,1024]{2,1,0:T(8,128)} reshape(f32[16,32,8,128]{3,2,1,0:T(8,128)} %bitcast.195) | data formatting | bytes 4194304 | tf_op jit(solution)/shard_map/reshape | solution.py:135
  180.5 3.9 %fusion.50 = f32[32,16,1024]{2,0,1:T(8,128)S(1)} fusion(f32[32,16,1024]{2,1,0:T(8,128)} %reshape.188), kind=kOutput, calls=%fused_computation.80 | convolution fusion | flops 100677632 | bytes 4194304 | tf_op jit(solution)/shard_map/kj,jmc->kmc/dot_general | solution.py:66
  184.5 2.5 multiply_subtract_fusion
  187.0 2.0 fusion.42
  189.0 2.0 fusion.40
  191.0 2.0 fusion.52
  193.0 2.2 fusion.55
  195.2 1.1 fusion.78
  196.4 1.1 fusion.82
  197.5 1.1 fusion.84
  198.6 1.1 fusion.80
  199.8 7.9 %fusion.17 = f32[32,16,1024]{2,0,1:T(8,128)S(1)} fusion(f32[32,16]{0,1:T(8,128)S(1)} %get-tuple-element.32, f32[32,16]{0,1:T(8,128)S(1)} %get-tuple-element.33, f32[16,32,1024]{2,0,1:T(8,128)S(1)} %fusion.80, f32[16,32,1024]{2,0,1:T(8,128)S(1)} %fusion.84, f32[16,32,1024]{2,0,1:T(8,128)S(1)} %fusion.82, f32[16,32,1024]{2,0,1:T(8,128)S(1)} %fusion.78), kind=kOutput, calls=%fused_computation.33 | convolution fusion | flops 103299072 | bytes 10489856 | tf_op jit(solution)/shard_map/kj,jmc->kmc/dot_general | solution.py:66
  207.7 7.7 %add_multiply_fusion = f32[32,16,1024]{2,0,1:T(8,128)S(1)} fusion(f32[32,16,1024]{2,0,1:T(8,128)S(1)} %fusion.17, f32[32,16]{0,1:T(8,128)S(1)} %get-tuple-element.32, f32[32,16]{0,1:T(8,128)S(1)} %get-tuple-element.33, f32[16,32,1024]{2,0,1:T(8,128)S(1)} %fusion.80, f32[16,32,1024]{2,0,1:T(8,128)S(1)} %fusion.84, f32[16,32,1024]{2,0,1:T(8,128)S(1)} %fusion.82, ...), kind=kOutput, calls=%fused_computation.54 | convolution fusion | flops 104348672 | bytes 12587008 | tf_op jit(solution)/shard_map/kj,jmc->kmc/dot_general | solution.py:66
  215.4 1.2 copy.88
  216.6 1.8 copy.93
  218.4 7.9 %all-to-all-start.1 = ((f32[512,8,128]{2,1,0:T(8,128)}), f32[512,8,128]{2,1,0:T(8,128)}, u32[]{:S(2)}, u32[]{:S(2)}) async-start(f32[512,8,128]{2,1,0:T(8,128)} %bitcast.196), calls=%async_computation.1 | async-start | bytes 4194304 | tf_op jit(solution)/shard_map/all_to_all | solution.py:136
  226.3 0.8 fusion.357
  227.1 4.6 %fusion.358 = (f32[32,16383]{1,0:T(8,128)}, f32[32,16383]{1,0:T(8,128)}, f32[32,16383]{1,0:T(8,128)}, f32[32,16383]{1,0:T(8,128)}) fusion(f32[32,16384]{1,0:T(8,128)S(1)} %copy-done, f32[1,16384]{1,0:T(1,128)S(1)} %collective-permute-done), kind=kLoop, calls=%fused_computation.388 | loop fusion | flops 1048512 | bytes 14745088 | tf_op jit(solution)/shard_map/jit(_roll_static)/slice | solution.py:148
  231.7 35.6 %all-to-all-done.1 = f32[512,8,128]{2,1,0:T(8,128)} async-done(((f32[512,8,128]{2,1,0:T(8,128)}), f32[512,8,128]{2,1,0:T(8,128)}, u32[]{:S(2)}, u32[]{:S(2)}) %all-to-all-start.1) | async-done | bytes 2097184 | tf_op jit(solution)/shard_map/all_to_all | solution.py:136
  267.3 3.0 %copy.89 = f32[32,8,16,128]{3,2,1,0:T(8,128)S(1)} copy(f32[32,8,16,128]{3,1,0,2:T(8,128)} %bitcast.36) | data formatting | bytes 4194304 | tf_op jit(solution)/shard_map/all_to_all | solution.py:136
  270.2 14.2 %fusion.11 = f32[32,16384]{1,0:T(8,128)} fusion(f32[32,16384]{1,0:T(8,128)S(1)} %copy-done, f32[1,16384]{1,0:T(1,128)S(1)} %collective-permute-done, f32[4,8,128,128]{3,2,1,0:T(8,128)S(1)} %bitcast.194, f32[33,16384]{1,0:T(8,128)S(1)} %copy-done.1, f32[32,16383]{1,0:T(8,128)} %get-tuple-element.15, f32[32,16383]{1,0:T(8,128)} %get-tuple-element.16, ...), kind=kLoop, calls=%fused_computation.17 | loop fusion | flops 14155776 | bytes 21036836 | tf_op jit(solution)/shard_map/add | solution.py:148
  (26 shorter events, 0.9 us)
Async XLA Ops:
  6.3 1.4 copy-start.4
  77.4 4.6 %copy-start = (f32[32,16384]{1,0:T(8,128)S(1)}, f32[32,16384]{1,0:T(8,128)}, u32[]{:S(2)}) copy-start(f32[32,16384]{1,0:T(8,128)} %param.4) | copy-start | bytes 6291460
  77.4 9.2 %copy-start.6 = (u32[32]{0:T(128)S(1)}, u32[32]{0:T(128)}, u32[]{:S(2)}) copy-start(u32[32]{0:T(128)} %constant.92) | copy-start | bytes 388
  77.4 10.4 %copy-start.5 = (f32[32]{0:T(128)S(1)}, f32[32]{0:T(128)}, u32[]{:S(2)}) copy-start(f32[32]{0:T(128)} %param.6) | copy-start | bytes 388
  77.4 78.7 %all-to-all-start = ((f32[16,1,32768]{2,1,0:T(1,128)}), f32[16,1,32768]{2,1,0:T(1,128)}, u32[]{:S(2)}, u32[]{:S(2)}) async-start(f32[16,1,32768]{2,1,0:T(1,128)} %reshape.203), calls=%async_computation | async-start | bytes 4194304 | tf_op jit(solution)/shard_map/all_to_all | solution.py:134
  82.1 144.9 %collective-permute-start = (f32[1,16384]{1,0:T(1,128)S(1)}, f32[1,16384]{1,0:T(1,128)S(1)}, u32[]{:S(2)}, u32[]{:S(2)}) collective-permute-start(f32[1,16384]{1,0:T(1,128)S(1)} %get-tuple-element.20), channel_id=1, source_target_pairs={{0,2},{2,4},{4,6},{6,8},{8,10},{10,12},{12,14},{14,16},{16,18},{18... | collective-permute-start | bytes 196616 | tf_op jit(solution)/shard_map/ppermute | solution.py:20
  82.4 66.4 %collective-permute-start.1 = (f32[1,16384]{1,0:T(1,128)S(1)}, f32[1,16384]{1,0:T(1,128)S(1)}, u32[]{:S(2)}, u32[]{:S(2)}) collective-permute-start(f32[1,16384]{1,0:T(1,128)S(1)} %get-tuple-element.19), channel_id=1, source_target_pairs={{2,0},{4,2},{6,4},{8,6},{10,8},{12,10},{14,12},{16,14},{18,16},{20... | collective-permute-start | bytes 196616 | tf_op jit(solution)/shard_map/ppermute | solution.py:22
  145.9 2.2 copy-start.3
  180.5 3.9 %copy-start.2 = (f32[32,16,1024]{2,1,0:T(8,128)S(1)}, f32[32,16,1024]{2,1,0:T(8,128)}, u32[]{:S(2)}) copy-start(f32[32,16,1024]{2,1,0:T(8,128)} %reshape.188) | copy-start | bytes 6291460
  218.4 48.9 %all-to-all-start.1 = ((f32[512,8,128]{2,1,0:T(8,128)}), f32[512,8,128]{2,1,0:T(8,128)}, u32[]{:S(2)}, u32[]{:S(2)}) async-start(f32[512,8,128]{2,1,0:T(8,128)} %bitcast.196), calls=%async_computation.1 | async-start | bytes 4194304 | tf_op jit(solution)/shard_map/all_to_all | solution.py:136
  267.3 3.0 %copy-start.1 = (f32[33,16384]{1,0:T(8,128)S(1)}, f32[33,16384]{1,0:T(8,128)}, u32[]{:S(2)}) copy-start(f32[33,16384]{1,0:T(8,128)} %dynamic-update-slice.2) | copy-start | bytes 6488068
where the time goes:
time: 290 us; the launch traced here: 285 us
  blocking collectives  80.5 us (28%)
  matrix products  69.3 us (24%)
  local copies, waits for them, and re-layouts  53.4 us (18%)
  waiting for transfers between devices  35.6 us (12%)
  other arithmetic  27.7 us (10%)
  starting transfers between devices  16.9 us (6%)
    dot_general x36, matrix products, contract(): jnp.einsum(form, left, right, precision=dft_precision, preferred_element_...  69.3 us
    unnamed x1, blocking collectives  56.8 us
    all_to_all x1, waiting for transfers between devices, body(): lax.all_to_all(convolve(shaped, column_filter, column_tables, column_form...  35.6 us
    all_gather x1, blocking collectives, body(): lax.all_gather(row_taps, 'rows', axis=0, tiled=True)  23.6 us
    unnamed x22, local copies, waits for them, and re-layouts  20.7 us
    add x1, other arithmetic, body(): filtered + stencil[offset_row, offset_col] * jnp.roll(row_band, 1 - offse...  14.2 us
    all_to_all x1, other arithmetic, body(): lax.all_to_all(blocks, 'rows', split_axis=2, concat_axis=0, tiled=True)  8.58 us
    all_to_all x1, starting transfers between devices, body(): lax.all_to_all(convolve(shaped, column_filter, column_tables, column_form...  7.86 us
  transfers between devices with their start and end apart: 4, of which 1 were waited for; matrix products, arithmetic and copies ran while one was open for 28% of the time, Pallas kernels for 0%

commit v1 on v0

--- a/solution.py
+++ b/solution.py
@@ -1,8 +1,12 @@
+import functools
 import math
 
 import jax
 import jax.numpy as jnp
+import numpy as np
 from jax import lax
+from jax.experimental import pallas as pl
+from jax.experimental.pallas import tpu as pltpu
 from jax.sharding import PartitionSpec as P
 
 dft_precision = lax.Precision.HIGH
@@ -151,6 +155,431 @@
     return filtered
 
 
+def split_bf16(values):
+    high = values.astype(jnp.bfloat16)
+    low = (values - high.astype(jnp.float32)).astype(jnp.bfloat16)
+    return high, low
+
+
+def mm(left, right):
+    return jnp.dot(left, right, preferred_element_type=jnp.float32)
+
+
+def mm3(left, right):
+    return mm(left[0], right[0]) + (mm(left[0], right[1]) + mm(left[1], right[0]))
+
+
+def host_tables(side):
+    length = side * side
+    index = np.arange(side)
+    product = index[:, None] * index[None, :]
+    angle = 2.0 * np.pi * (product % side) / side
+    cos, sin = np.cos(angle), np.sin(angle)
+    table = np.block([[cos, sin], [-sin, cos]]).astype(np.float32)
+
+    def halves(array):
+        high = array.astype(jnp.bfloat16)
+        low = (array - high.astype(np.float32)).astype(jnp.bfloat16)
+        return high, low
+
+    fwd_high, fwd_low = halves(table)
+    inv_high, inv_low = halves(np.ascontiguousarray(table.T))
+    turn = 2.0 * np.pi * product / length
+    return (
+        fwd_high,
+        fwd_low,
+        inv_high,
+        inv_low,
+        np.cos(turn).astype(np.float32),
+        (-np.sin(turn)).astype(np.float32),
+    )
+
+
+def kernel(
+    dims,
+    pixels,
+    top_row,
+    bottom_row,
+    taps,
+    stencil,
+    fwd_high,
+    fwd_low,
+    inv_high,
+    inv_low,
+    twist_real,
+    twist_imag,
+    out,
+    recv,
+    recv_high,
+    recv_low,
+    ready,
+    back,
+    padded,
+    halo_above,
+    halo_below,
+    all_taps,
+    circ_high,
+    circ_low,
+    filter_real,
+    filter_imag,
+    send_px,
+    recv_px,
+    send_tap,
+    recv_tap,
+    send_halo,
+    recv_halo,
+    send_back,
+    recv_back,
+    local_sem,
+):
+    count, rows_dev, side = dims
+    groups = rows_dev // 8
+    cols_dev = side * side // count
+    a_dev = cols_dev // 128
+    column_length = count * rows_dev
+    tap_rows = taps.shape[0]
+    row_tap_rows = a_dev
+    me = lax.axis_index("rows")
+
+    def peer(step):
+        return lax.rem(me + step, count)
+
+    def source(step):
+        return lax.rem(me + count - step, count)
+
+    barrier = pltpu.get_barrier_semaphore()
+
+    @pl.loop(1, count)
+    def _(step):
+        pl.semaphore_signal(barrier, inc=1, device_id={"rows": peer(step)})
+
+    pl.semaphore_wait(barrier, count - 1)
+
+    def px_copy(step):
+        to = peer(step)
+        return pltpu.make_async_remote_copy(
+            src_ref=pixels.at[:, pl.ds(pl.multiple_of(to * cols_dev, 128), cols_dev)],
+            dst_ref=recv.at[pl.ds(pl.multiple_of(me * rows_dev, 8), rows_dev), :],
+            send_sem=send_px.at[step],
+            recv_sem=recv_px.at[step],
+            device_id={"rows": to},
+        )
+
+    def tap_copy(step):
+        return pltpu.make_async_remote_copy(
+            src_ref=taps,
+            dst_ref=all_taps.at[me],
+            send_sem=send_tap.at[step],
+            recv_sem=recv_tap.at[step],
+            device_id={"rows": peer(step)},
+        )
+
+    def halo_copy(which):
+        return pltpu.make_async_remote_copy(
+            src_ref=(bottom_row, top_row)[which],
+            dst_ref=(halo_above, halo_below)[which],
+            send_sem=send_halo.at[which],
+            recv_sem=recv_halo.at[which],
+            device_id={"rows": peer(1 if which == 0 else count - 1)},
+        )
+
+    @pl.loop(1, count)
+    def _(step):
+        tap_copy(step).start()
+
+    halo_copy(0).start()
+    halo_copy(1).start()
+
+    @pl.loop(1, count)
+    def _(step):
+        px_copy(step).start()
+
+    own_px = pltpu.make_async_copy(
+        pixels.at[:, pl.ds(pl.multiple_of(me * cols_dev, 128), cols_dev)],
+        recv.at[pl.ds(pl.multiple_of(me * rows_dev, 8), rows_dev), :],
+        local_sem.at[0],
+    )
+    own_px.start()
+    own_tap = pltpu.make_async_copy(taps, all_taps.at[me], local_sem.at[1])
+    own_tap.start()
+
+    padded[8 : 8 + rows_dev, :] = pixels[...]
+    halo_copy(0).wait_recv()
+    halo_copy(1).wait_recv()
+    padded[7:8, :] = halo_above[...]
+    padded[8 + rows_dev : 9 + rows_dev, :] = halo_below[...]
+    width = side * side
+    for group in range(groups):
+        base = group * 8
+        above = padded[7 + base : 15 + base, :]
+        here = padded[8 + base : 16 + base, :]
+        below = padded[9 + base : 17 + base, :]
+        sums = [
+            stencil[0, b] * above + stencil[1, b] * here + stencil[2, b] * below for b in range(3)
+        ]
+        out[base : base + 8, :] = (
+            sums[1] + pltpu.roll(sums[0], 1, 1) + pltpu.roll(sums[2], width - 1, 1)
+        )
+
+    own_tap.wait()
+
+    @pl.loop(1, count)
+    def _(step):
+        tap_copy(step).wait_recv()
+
+    tap_sum = all_taps[0, row_tap_rows:tap_rows, :]
+    for rank in range(1, count):
+        tap_sum = tap_sum + all_taps[rank, row_tap_rows:tap_rows, :]
+    line = jnp.concatenate(
+        [tap_sum[j : j + 1, :] for j in range(column_length // 128)], axis=1
+    )
+    per_block = 128 // rows_dev
+    line = jnp.broadcast_to(line, (128, column_length))
+    turned = [
+        pltpu.roll(line, block * 128, 1, stride=1, stride_axis=0)
+        for block in range(column_length // 128)
+    ]
+    for group in range(groups):
+        part = jnp.concatenate(
+            [
+                turned[rank // per_block][
+                    (rank % per_block) * rows_dev + group * 8 :
+                    (rank % per_block) * rows_dev + group * 8 + 8
+                ]
+                for rank in range(count)
+            ],
+            axis=0,
+        )
+        high, low = split_bf16(part)
+        circ_high[group] = high
+        circ_low[group] = low
+
+    forward_table = (fwd_high, fwd_low)
+    inverse_table = (inv_high, inv_low)
+
+    def loaded(table):
+        return (table[0][...], table[1][...])
+
+    def swap(real, imag):
+        return jnp.concatenate(
+            [
+                jnp.concatenate([real[:, :side], imag[:, :side]], axis=1),
+                jnp.concatenate([real[:, side:], imag[:, side:]], axis=1),
+            ],
+            axis=0,
+        )
+
+    def spectrum(cells):
+        first = mm3(loaded(forward_table), split_bf16(cells))
+        real, imag = first[:side], first[side:]
+        turn_r = jnp.concatenate([twist_real[...]] * 2, axis=1)
+        turn_i = jnp.concatenate([twist_imag[...]] * 2, axis=1)
+        turned_cells = swap(real * turn_r - imag * turn_i, real * turn_i + imag * turn_r)
+        return mm3(split_bf16(turned_cells), loaded(inverse_table))
+
+    def inverse_of(real, imag):
+        cells = jnp.concatenate([real, imag], axis=1)
+        first = mm3(split_bf16(cells), loaded(forward_table))
+        real, imag = first[:, :side], first[:, side:]
+        turn_r = jnp.concatenate([twist_real[...]] * 2, axis=0)
+        turn_i = jnp.concatenate([twist_imag[...]] * 2, axis=0)
+        back_real = real * turn_r + imag * turn_i
+        back_imag = imag * turn_r - real * turn_i
+        cells = jnp.concatenate(
+            [
+                jnp.concatenate([back_real[:side], back_real[side:]], axis=1),
+                jnp.concatenate([back_imag[:side], back_imag[side:]], axis=1),
+            ],
+            axis=0,
+        )
+        return mm3(loaded(inverse_table), split_bf16(cells))
+
+    row_filter = jnp.concatenate(
+        [all_taps[rank, 0:row_tap_rows, :] for rank in range(count)], axis=0
+    )
+    nothing = jnp.zeros_like(row_filter)
+    filter_spec = spectrum(
+        jnp.concatenate(
+            [
+                jnp.concatenate([row_filter, nothing], axis=1),
+                jnp.concatenate([nothing, nothing], axis=1),
+            ],
+            axis=0,
+        )
+    )[:side]
+    filter_real[...] = filter_spec[:, :side] * (1.0 / (side * side))
+    filter_imag[...] = filter_spec[:, side:] * (1.0 / (side * side))
+
+    def take(rank):
+        at = pl.ds(pl.multiple_of(rank * rows_dev, 16), rows_dev)
+        high, low = split_bf16(recv[at, :])
+        recv_high[at, :] = high
+        recv_low[at, :] = low
+
+    own_px.wait()
+    take(me)
+
+    @pl.loop(1, count)
+    def _(step):
+        px_copy(step).wait_recv()
+        take(source(step))
+
+    flat_ready = ready.reshape(groups * count * 8 * a_dev, 128)
+
+    def back_copy(group, step):
+        to = peer(step)
+        return pltpu.make_async_remote_copy(
+            src_ref=ready.at[pl.ds((group * count + to) * 8, 8)],
+            dst_ref=back.at[pl.ds(group * 8, 8), pl.ds(pl.multiple_of(me * a_dev, 8), a_dev), :],
+            send_sem=send_back.at[group, step],
+            recv_sem=recv_back.at[group, step],
+            device_id={"rows": to},
+        )
+
+    def own_back(group):
+        return pltpu.make_async_copy(
+            ready.at[pl.ds((group * count + me) * 8, 8)],
+            back.at[pl.ds(group * 8, 8), pl.ds(pl.multiple_of(me * a_dev, 8), a_dev), :],
+            local_sem.at[2 + group],
+        )
+
+    tile = 256
+    for group in range(groups):
+        for piece in range(cols_dev // tile):
+            cut = slice(piece * tile, (piece + 1) * tile)
+            done = mm3(
+                (circ_high[group], circ_low[group]), (recv_high[:, cut], recv_low[:, cut])
+            )
+            for j in range(tile // 128):
+                flat_ready[
+                    pl.ds(group * count * 8 * a_dev + piece * (tile // 128) + j, count * 8, stride=a_dev), :
+                ] = done[:, j * 128 : (j + 1) * 128]
+
+        @pl.loop(1, count)
+        def _(step, group=group):
+            back_copy(group, step).start()
+
+        own_back(group).start()
+
+    flat_back = back.reshape(rows_dev * side, side)
+    for group in range(groups):
+        own_back(group).wait()
+
+        @pl.loop(1, count)
+        def _(step, group=group):
+            back_copy(group, step).wait_recv()
+
+        for half in range(2):
+            row = group * 8 + half * 4
+            cells = jnp.concatenate(
+                [
+                    jnp.concatenate([back[row], back[row + 2]], axis=1),
+                    jnp.concatenate([back[row + 1], back[row + 3]], axis=1),
+                ],
+                axis=0,
+            )
+            spec = spectrum(cells)
+            real, imag = spec[:, :side], spec[:, side:]
+            filt_r = jnp.concatenate([filter_real[...]] * 2, axis=0)
+            filt_i = jnp.concatenate([filter_imag[...]] * 2, axis=0)
+            done = inverse_of(real * filt_r - imag * filt_i, real * filt_i + imag * filt_r)
+            back[row] = done[:side, :side]
+            back[row + 1] = done[side:, :side]
+            back[row + 2] = done[:side, side:]
+            back[row + 3] = done[side:, side:]
+        for a in range(side):
+            cut = slice(a * side, (a + 1) * side)
+            out[group * 8 : group * 8 + 8, cut] += flat_back[
+                pl.ds(group * 8 * side + a, 8, stride=side), :
+            ]
+
+    halo_copy(0).wait_send()
+    halo_copy(1).wait_send()
+
+    @pl.loop(1, count)
+    def _(step):
+        tap_copy(step).wait_send()
+        px_copy(step).wait_send()
+        for group in range(groups):
+            back_copy(group, step).wait_send()
+
+
+def fits(pixels, row_taps, column_taps):
+    rows_dev, row_length = pixels.shape
+    count = lax.axis_size("rows")
+    side = math.isqrt(row_length)
+    return (
+        side == 128
+        and side * side == row_length
+        and row_length % (count * 1024) == 0
+        and rows_dev % 16 == 0
+        and 128 % rows_dev == 0
+        and (count * rows_dev) % 128 == 0
+    )
+
+
+def fused(pixels, row_taps, column_taps, stencil):
+    rows_dev, row_length = pixels.shape
+    count = lax.axis_size("rows")
+    side = math.isqrt(row_length)
+    column_length = rows_dev * count
+    cols_dev = row_length // count
+    a_dev = cols_dev // 128
+    groups = rows_dev // 8
+    me = lax.axis_index("rows")
+    slots = -(-column_length // 1024) * 1024
+    wanted = (column_length - jnp.arange(slots, dtype=jnp.int32)) % column_length
+    wanted = jnp.where(jnp.arange(slots) < column_length, wanted, -1)
+    held = me * rows_dev + jnp.arange(rows_dev, dtype=jnp.int32)
+    placed = jnp.sum(
+        jnp.where(wanted[:, None] == held[None, :], column_taps[None, :], 0.0), axis=1
+    )
+    taps = jnp.concatenate([row_taps.reshape(a_dev, 128), placed.reshape(slots // 128, 128)])
+    tables = [jnp.asarray(table) for table in host_tables(side)]
+    vmem = pl.BlockSpec(memory_space=pltpu.VMEM)
+    f32, bf16 = jnp.float32, jnp.bfloat16
+    dma = pltpu.SemaphoreType.DMA
+    return pl.pallas_call(
+        functools.partial(kernel, (count, rows_dev, side)),
+        out_shape=jax.ShapeDtypeStruct(pixels.shape, f32),
+        in_specs=[vmem] * 4 + [pl.BlockSpec(memory_space=pltpu.SMEM)] + [vmem] * 6,
+        out_specs=vmem,
+        scratch_shapes=[
+            pltpu.VMEM((column_length, cols_dev), f32),
+            pltpu.VMEM((column_length, cols_dev), bf16),
+            pltpu.VMEM((column_length, cols_dev), bf16),
+            pltpu.VMEM((column_length, a_dev, 128), f32),
+            pltpu.VMEM((rows_dev, side, side), f32),
+            pltpu.VMEM((rows_dev + 16, row_length), f32),
+            pltpu.VMEM((1, row_length), f32),
+            pltpu.VMEM((1, row_length), f32),
+            pltpu.VMEM((count,) + taps.shape, f32),
+            pltpu.VMEM((groups, count * 8, column_length), bf16),
+            pltpu.VMEM((groups, count * 8, column_length), bf16),
+            pltpu.VMEM((side, side), f32),
+            pltpu.VMEM((side, side), f32),
+            dma((count,)),
+            dma((count,)),
+            dma((count,)),
+            dma((count,)),
+            dma((2,)),
+            dma((2,)),
+            dma((groups, count)),
+            dma((groups, count)),
+            dma((2 + groups,)),
+        ],
+        compiler_params=pltpu.CompilerParams(
+            collective_id=0, has_side_effects=True, vmem_limit_bytes=48 * 1024 * 1024
+        ),
+    )(pixels, pixels[:1], pixels[rows_dev - 1 :], taps, stencil, *tables)
+
+
+def chosen(pixels, row_taps, column_taps, stencil):
+    if fits(pixels, row_taps, column_taps):
+        return fused(pixels, row_taps, column_taps, stencil)
+    return body(pixels, row_taps, column_taps, stencil)
+
+
 def solution(mesh):
     in_specs = (
         P(("chan", "rows"), None),
@@ -159,4 +588,4 @@
         P("chan", None),
     )
     out_specs = P(("chan", "rows"), None)
-    return jax.shard_map(body, mesh=mesh, in_specs=in_specs, out_specs=out_specs, check_vma=False)
+    return jax.shard_map(chosen, mesh=mesh, in_specs=in_specs, out_specs=out_specs, check_vma=False)

time: 290 us -> 122 us (0.42); the launches traced: 285 us -> 122 us
  Pallas kernels: 0 us -> 110 us
  blocking collectives: 80.5 us -> 0 us
  matrix products: 69.3 us -> 0 us
  local copies, waits for them, and re-layouts: 53.4 us -> 10.2 us
  waiting for transfers between devices: 35.6 us -> 0 us
  other arithmetic: 27.7 us -> 1.45 us
  starting transfers between devices: 16.9 us -> 0 us
    pallas_call x0 -> x1, Pallas kernels: none -> 110 us  [fused(): pl.pallas_call(functools.partial(kernel, (count, rows_dev, side)), out_sh...]
    dot_general x36 -> x0, matrix products: 69.3 us -> none  [contract(): jnp.einsum(form, left, right, precision=dft_precision, preferred_element_...]
    unnamed x1 -> x0, blocking collectives: 56.8 us -> none
    all_to_all x2 -> x0, waiting for transfers between devices: 35.6 us -> none  [the longest x1 35.6 us: body(): lax.all_to_all(convolve(shaped, column_filter, column_tables, column_form...]
    all_gather x1 -> x0, blocking collectives: 23.6 us -> none  [body(): lax.all_gather(row_taps, 'rows', axis=0, tiled=True)]
    add x1, other arithmetic: 14.2 us -> 0.01 us  [fused(): held = me * rows_dev + jnp.arange(rows_dev, dtype=jnp.int32)]
    all_to_all x2 -> x0, starting transfers between devices: 12.4 us -> none  [the longest x1 7.86 us: body(): lax.all_to_all(convolve(shaped, column_filter, column_tables, column_form...]
    unnamed x22 -> x17, local copies, waits for them, and re-layouts: 20.7 us -> 8.88 us
  transfers between devices with their start and end apart: 4 -> 0, of which waited for: 1 -> 0; matrix products, arithmetic and copies ran while one was open for 28% -> 0% of each run, Pallas kernels for 0% -> 0%
where the time goes in v1:
time: 122 us
  Pallas kernels  110 us (90%)
  local copies, waits for them, and re-layouts  10.2 us (8%)
  other arithmetic  1.45 us (1%)
    pallas_call x1, Pallas kernels, fused(): pl.pallas_call(functools.partial(kernel, (count, rows_dev, side)), out_sh...  110 us
    unnamed x17, local copies, waits for them, and re-layouts  8.88 us

profile of v1, /device:TPU:0, one launch (start us, length us, event | category | flops | bytes accessed | tf_op | source)
XLA Modules:
  0.0 122.0 jit_solution(309552796531034643)
XLA Ops:
  0.0 0.7 select_reduce_fusion
  0.8 0.7 pad_maximum_fusion.taps
  1.5 1.3 %fusion.5 = (f32[1,16384]{1,0:T(1,128)S(1)}, f32[1,16384]{1,0:T(1,128)S(1)}) fusion(f32[32,16384]{1,0:T(8,128)} %pixels.1), kind=kLoop, calls=%fused_computation.12 | loop fusion | bytes 262144 | tf_op jit(solution)/shard_map/slice | solution.py:574
  2.7 0.0 copy-start
  2.8 1.6 %copy-done = f32[32,16384]{1,0:T(8,128)S(1)} copy-done((f32[32,16384]{1,0:T(8,128)S(1)}, f32[32,16384]{1,0:T(8,128)}, u32[]{:S(2)}) %copy-start) | copy-done | bytes 2097176
  4.3 0.0 copy-start.1
  4.3 0.9 copy-done.1
  5.2 0.0 copy-start.2
  5.3 0.9 copy-done.2
  6.2 0.0 copy-start.3
  6.2 0.9 copy-done.3
  7.1 0.0 copy-start.4
  7.1 0.9 copy-done.4
  8.0 0.0 copy-start.5
  8.0 0.8 copy-done.5
  8.8 0.0 copy-start.6
  8.8 0.8 copy-done.6
  9.6 0.0 copy-start.7
  9.6 0.7 copy-done.7
  10.3 110.4 %shard_map.100 = f32[32,16384]{1,0:T(8,128)S(1)} custom-call(f32[32,16384]{1,0:T(8,128)S(1)} %copy-done, f32[1,16384]{1,0:T(1,128)S(1)} %get-tuple-element.6.top_row, f32[1,16384]{1,0:T(1,128)S(1)} %get-tuple-element.5.bottom_row, f32[16,128]{1,0:T(8,128)S(1)} %pad_maximum_fusion.taps, f32[3,3]{1,0:T(4,128)S(1)} %copy-done.7, ...), custom_call_target="tpu_custom_call" | custom-call | tf_op jit(solution)/shard_map/pallas_call | solution.py:542
  120.7 1.3 %copy.12 = f32[32,16384]{1,0:T(8,128)} copy(f32[32,16384]{1,0:T(8,128)S(1)} %shard_map.100) | data formatting | bytes 4194304
  (2 shorter events, 0.0 us)
Async XLA Ops:
  2.7 1.6 %copy-start = (f32[32,16384]{1,0:T(8,128)S(1)}, f32[32,16384]{1,0:T(8,128)}, u32[]{:S(2)}) copy-start(f32[32,16384]{1,0:T(8,128)} %pixels.1) | copy-start | bytes 6291460
  4.3 0.9 copy-start.1
  5.2 0.9 copy-start.2
  6.2 0.9 copy-start.3
  7.1 0.9 copy-start.4
  8.0 0.8 copy-start.5
  8.8 0.8 copy-start.6
  9.6 0.7 copy-start.7

commit v2 on v1

--- a/solution.py
+++ b/solution.py
@@ -198,47 +198,52 @@
 def kernel(
     dims,
     pixels,
+    row_taps,
+    column_taps,
+    stencil,
+    tables_in,
+    twists_in,
+    out,
+    padded,
+    tables,
+    twists,
     top_row,
     bottom_row,
-    taps,
-    stencil,
-    fwd_high,
-    fwd_low,
-    inv_high,
-    inv_low,
-    twist_real,
-    twist_imag,
-    out,
     recv,
     recv_high,
     recv_low,
     ready,
     back,
-    padded,
+    cells_by_row,
     halo_above,
     halo_below,
-    all_taps,
+    all_row,
+    all_column,
     circ_high,
     circ_low,
     filter_real,
     filter_imag,
     send_px,
     recv_px,
-    send_tap,
-    recv_tap,
+    send_row,
+    recv_row,
+    send_col,
+    recv_col,
     send_halo,
     recv_halo,
     send_back,
     recv_back,
+    send_last,
+    recv_last,
     local_sem,
 ):
-    count, rows_dev, side = dims
+    count, rows_dev, side, pieces = dims
     groups = rows_dev // 8
     cols_dev = side * side // count
     a_dev = cols_dev // 128
     column_length = count * rows_dev
-    tap_rows = taps.shape[0]
-    row_tap_rows = a_dev
+    piece_cols = cols_dev // pieces
+    own = slice(8, 8 + rows_dev)
     me = lax.axis_index("rows")
 
     def peer(step):
@@ -246,6 +251,13 @@
 
     def source(step):
         return lax.rem(me + count - step, count)
+
+    load_px = pltpu.make_async_copy(pixels, padded.at[own, :], local_sem.at[0])
+    load_tables = pltpu.make_async_copy(tables_in, tables, local_sem.at[1])
+    load_twists = pltpu.make_async_copy(twists_in, twists, local_sem.at[2])
+    load_px.start()
+    load_tables.start()
+    load_twists.start()
 
     barrier = pltpu.get_barrier_semaphore()
 
@@ -255,22 +267,37 @@
 
     pl.semaphore_wait(barrier, count - 1)
 
-    def px_copy(step):
+    def columns_of(rank, piece):
+        return pl.ds(pl.multiple_of(rank * cols_dev + piece * piece_cols, 128), piece_cols)
+
+    def rows_of(rank):
+        return pl.ds(pl.multiple_of(rank * rows_dev, 16), rows_dev)
+
+    def px_copy(piece, step):
         to = peer(step)
         return pltpu.make_async_remote_copy(
-            src_ref=pixels.at[:, pl.ds(pl.multiple_of(to * cols_dev, 128), cols_dev)],
-            dst_ref=recv.at[pl.ds(pl.multiple_of(me * rows_dev, 8), rows_dev), :],
-            send_sem=send_px.at[step],
-            recv_sem=recv_px.at[step],
+            src_ref=padded.at[own, columns_of(to, piece)],
+            dst_ref=recv.at[piece, rows_of(me), :],
+            send_sem=send_px.at[piece, step],
+            recv_sem=recv_px.at[piece, step],
             device_id={"rows": to},
         )
 
-    def tap_copy(step):
+    def row_copy(step):
         return pltpu.make_async_remote_copy(
-            src_ref=taps,
-            dst_ref=all_taps.at[me],
-            send_sem=send_tap.at[step],
-            recv_sem=recv_tap.at[step],
+            src_ref=row_taps,
+            dst_ref=all_row.at[me],
+            send_sem=send_row.at[step],
+            recv_sem=recv_row.at[step],
+            device_id={"rows": peer(step)},
+        )
+
+    def col_copy(step):
+        return pltpu.make_async_remote_copy(
+            src_ref=column_taps,
+            dst_ref=all_column.at[me],
+            send_sem=send_col.at[step],
+            recv_sem=recv_col.at[step],
             device_id={"rows": peer(step)},
         )
 
@@ -283,60 +310,48 @@
             device_id={"rows": peer(1 if which == 0 else count - 1)},
         )
 
+    load_px.wait()
+
     @pl.loop(1, count)
     def _(step):
-        tap_copy(step).start()
-
+        px_copy(0, step).start()
+        col_copy(step).start()
+
+    top_row[...] = padded[8:9, :]
+    bottom_row[...] = padded[7 + rows_dev : 8 + rows_dev, :]
     halo_copy(0).start()
     halo_copy(1).start()
 
     @pl.loop(1, count)
     def _(step):
-        px_copy(step).start()
-
-    own_px = pltpu.make_async_copy(
-        pixels.at[:, pl.ds(pl.multiple_of(me * cols_dev, 128), cols_dev)],
-        recv.at[pl.ds(pl.multiple_of(me * rows_dev, 8), rows_dev), :],
-        local_sem.at[0],
-    )
-    own_px.start()
-    own_tap = pltpu.make_async_copy(taps, all_taps.at[me], local_sem.at[1])
-    own_tap.start()
-
-    padded[8 : 8 + rows_dev, :] = pixels[...]
-    halo_copy(0).wait_recv()
-    halo_copy(1).wait_recv()
-    padded[7:8, :] = halo_above[...]
-    padded[8 + rows_dev : 9 + rows_dev, :] = halo_below[...]
-    width = side * side
-    for group in range(groups):
-        base = group * 8
-        above = padded[7 + base : 15 + base, :]
-        here = padded[8 + base : 16 + base, :]
-        below = padded[9 + base : 17 + base, :]
-        sums = [
-            stencil[0, b] * above + stencil[1, b] * here + stencil[2, b] * below for b in range(3)
-        ]
-        out[base : base + 8, :] = (
-            sums[1] + pltpu.roll(sums[0], 1, 1) + pltpu.roll(sums[2], width - 1, 1)
-        )
-
-    own_tap.wait()
+        row_copy(step).start()
+
+    for piece in range(1, pieces):
+
+        @pl.loop(1, count)
+        def _(step, piece=piece):
+            px_copy(piece, step).start()
+
+    all_row[me] = row_taps[...]
+    all_column[me] = column_taps[...]
+    load_tables.wait()
+    load_twists.wait()
 
     @pl.loop(1, count)
     def _(step):
-        tap_copy(step).wait_recv()
-
-    tap_sum = all_taps[0, row_tap_rows:tap_rows, :]
-    for rank in range(1, count):
-        tap_sum = tap_sum + all_taps[rank, row_tap_rows:tap_rows, :]
-    line = jnp.concatenate(
-        [tap_sum[j : j + 1, :] for j in range(column_length // 128)], axis=1
-    )
+        col_copy(step).wait_recv()
+
     per_block = 128 // rows_dev
+    lines = []
+    for block in reversed(range(column_length // 128)):
+        total = all_column[block * per_block]
+        for rank in range(block * per_block + 1, (block + 1) * per_block):
+            total = total + all_column[rank]
+        lines.append(total)
+    line = jnp.concatenate(lines, axis=1)
     line = jnp.broadcast_to(line, (128, column_length))
     turned = [
-        pltpu.roll(line, block * 128, 1, stride=1, stride_axis=0)
+        pltpu.roll(line, block * 128 + 1, 1, stride=1, stride_axis=0)
         for block in range(column_length // 128)
     ]
     for group in range(groups):
@@ -354,11 +369,11 @@
         circ_high[group] = high
         circ_low[group] = low
 
-    forward_table = (fwd_high, fwd_low)
-    inverse_table = (inv_high, inv_low)
+    forward_table = (0, 1)
+    inverse_table = (2, 3)
 
     def loaded(table):
-        return (table[0][...], table[1][...])
+        return (tables[table[0]], tables[table[1]])
 
     def swap(real, imag):
         return jnp.concatenate(
@@ -372,8 +387,8 @@
     def spectrum(cells):
         first = mm3(loaded(forward_table), split_bf16(cells))
         real, imag = first[:side], first[side:]
-        turn_r = jnp.concatenate([twist_real[...]] * 2, axis=1)
-        turn_i = jnp.concatenate([twist_imag[...]] * 2, axis=1)
+        turn_r = jnp.concatenate([twists[0]] * 2, axis=1)
+        turn_i = jnp.concatenate([twists[1]] * 2, axis=1)
         turned_cells = swap(real * turn_r - imag * turn_i, real * turn_i + imag * turn_r)
         return mm3(split_bf16(turned_cells), loaded(inverse_table))
 
@@ -381,8 +396,8 @@
         cells = jnp.concatenate([real, imag], axis=1)
         first = mm3(split_bf16(cells), loaded(forward_table))
         real, imag = first[:, :side], first[:, side:]
-        turn_r = jnp.concatenate([twist_real[...]] * 2, axis=0)
-        turn_i = jnp.concatenate([twist_imag[...]] * 2, axis=0)
+        turn_r = jnp.concatenate([twists[0]] * 2, axis=0)
+        turn_i = jnp.concatenate([twists[1]] * 2, axis=0)
         back_real = real * turn_r + imag * turn_i
         back_imag = imag * turn_r - real * turn_i
         cells = jnp.concatenate(
@@ -394,87 +409,132 @@
         )
         return mm3(loaded(inverse_table), split_bf16(cells))
 
-    row_filter = jnp.concatenate(
-        [all_taps[rank, 0:row_tap_rows, :] for rank in range(count)], axis=0
-    )
-    nothing = jnp.zeros_like(row_filter)
-    filter_spec = spectrum(
-        jnp.concatenate(
-            [
-                jnp.concatenate([row_filter, nothing], axis=1),
-                jnp.concatenate([nothing, nothing], axis=1),
-            ],
-            axis=0,
-        )
-    )[:side]
-    filter_real[...] = filter_spec[:, :side] * (1.0 / (side * side))
-    filter_imag[...] = filter_spec[:, side:] * (1.0 / (side * side))
-
-    def take(rank):
-        at = pl.ds(pl.multiple_of(rank * rows_dev, 16), rows_dev)
-        high, low = split_bf16(recv[at, :])
-        recv_high[at, :] = high
-        recv_low[at, :] = low
-
-    own_px.wait()
-    take(me)
-
-    @pl.loop(1, count)
-    def _(step):
-        px_copy(step).wait_recv()
-        take(source(step))
-
-    flat_ready = ready.reshape(groups * count * 8 * a_dev, 128)
-
-    def back_copy(group, step):
+    def filter_spectrum():
+        @pl.loop(1, count)
+        def _(step):
+            row_copy(step).wait_recv()
+
+        row_filter = jnp.concatenate([all_row[rank] for rank in range(count)], axis=0)
+        nothing = jnp.zeros_like(row_filter)
+        filter_spec = spectrum(
+            jnp.concatenate(
+                [
+                    jnp.concatenate([row_filter, nothing], axis=1),
+                    jnp.concatenate([nothing, nothing], axis=1),
+                ],
+                axis=0,
+            )
+        )[:side]
+        filter_real[...] = filter_spec[:, :side] * (1.0 / (side * side))
+        filter_imag[...] = filter_spec[:, side:] * (1.0 / (side * side))
+
+    def add_stencil():
+        halo_copy(0).wait_recv()
+        halo_copy(1).wait_recv()
+        padded[7:8, :] = halo_above[...]
+        padded[8 + rows_dev : 9 + rows_dev, :] = halo_below[...]
+        width = side * side
+        for group in range(groups):
+            base = group * 8
+            above = padded[7 + base : 15 + base, :]
+            here = padded[8 + base : 16 + base, :]
+            below = padded[9 + base : 17 + base, :]
+            sums = [
+                stencil[0, b] * above + stencil[1, b] * here + stencil[2, b] * below
+                for b in range(3)
+            ]
+            out[base : base + 8, :] = (
+                sums[1] + pltpu.roll(sums[0], 1, 1) + pltpu.roll(sums[2], width - 1, 1)
+            )
+
+    def back_copy(piece, step):
         to = peer(step)
         return pltpu.make_async_remote_copy(
-            src_ref=ready.at[pl.ds((group * count + to) * 8, 8)],
-            dst_ref=back.at[pl.ds(group * 8, 8), pl.ds(pl.multiple_of(me * a_dev, 8), a_dev), :],
-            send_sem=send_back.at[group, step],
-            recv_sem=recv_back.at[group, step],
+            src_ref=ready.at[piece, rows_of(to), :],
+            dst_ref=back.at[:, columns_of(me, piece)],
+            send_sem=send_back.at[piece, step],
+            recv_sem=recv_back.at[piece, step],
             device_id={"rows": to},
         )
 
-    def own_back(group):
-        return pltpu.make_async_copy(
-            ready.at[pl.ds((group * count + me) * 8, 8)],
-            back.at[pl.ds(group * 8, 8), pl.ds(pl.multiple_of(me * a_dev, 8), a_dev), :],
-            local_sem.at[2 + group],
-        )
-
-    tile = 256
+    last = pieces - 1
+
+    def last_copy(group, step):
+        to = peer(step)
+        return pltpu.make_async_remote_copy(
+            src_ref=ready.at[last, pl.ds(pl.multiple_of(to * rows_dev + group * 8, 8), 8), :],
+            dst_ref=back.at[pl.ds(group * 8, 8), columns_of(me, last)],
+            send_sem=send_last.at[group, step],
+            recv_sem=recv_last.at[group, step],
+            device_id={"rows": to},
+        )
+
+    def take(piece, rank, values):
+        at = rows_of(rank)
+        high, low = split_bf16(values)
+        recv_high[piece, at, :] = high
+        recv_low[piece, at, :] = low
+
+    def filtered_rows(piece, group):
+        return mm3(
+            (circ_high[group], circ_low[group]), (recv_high[piece], recv_low[piece])
+        )
+
+    for piece in range(pieces):
+        take(piece, me, padded[own, columns_of(me, piece)])
+
+    for piece in range(pieces):
+
+        @pl.loop(1, count)
+        def _(step, piece=piece):
+            px_copy(piece, step).wait_recv()
+            take(piece, source(step), recv[piece, rows_of(source(step)), :])
+
+        for group in range(groups):
+            done = filtered_rows(piece, group)
+            for rank in range(count):
+                at = rank * rows_dev + group * 8
+                ready[piece, at : at + 8, :] = done[rank * 8 : rank * 8 + 8]
+            if piece == last:
+
+                @pl.loop(1, count)
+                def _(step, group=group):
+                    last_copy(group, step).start()
+
+        if piece != last:
+
+            @pl.loop(1, count)
+            def _(step, piece=piece):
+                back_copy(piece, step).start()
+
+        back[:, columns_of(me, piece)] = ready[piece, rows_of(me), :]
+        if piece == 0:
+            filter_spectrum()
+            add_stencil()
+
+    flat_cells = cells_by_row.reshape(rows_dev * side, side)
+    for piece in range(last):
+
+        @pl.loop(1, count)
+        def _(step, piece=piece):
+            back_copy(piece, step).wait_recv()
+
     for group in range(groups):
-        for piece in range(cols_dev // tile):
-            cut = slice(piece * tile, (piece + 1) * tile)
-            done = mm3(
-                (circ_high[group], circ_low[group]), (recv_high[:, cut], recv_low[:, cut])
-            )
-            for j in range(tile // 128):
-                flat_ready[
-                    pl.ds(group * count * 8 * a_dev + piece * (tile // 128) + j, count * 8, stride=a_dev), :
-                ] = done[:, j * 128 : (j + 1) * 128]
 
         @pl.loop(1, count)
         def _(step, group=group):
-            back_copy(group, step).start()
-
-        own_back(group).start()
-
-    flat_back = back.reshape(rows_dev * side, side)
-    for group in range(groups):
-        own_back(group).wait()
-
-        @pl.loop(1, count)
-        def _(step, group=group):
-            back_copy(group, step).wait_recv()
-
+            last_copy(group, step).wait_recv()
+
+        for a in range(side):
+            flat_cells[pl.ds(group * 8 * side + a, 8, stride=side), :] = back[
+                group * 8 : group * 8 + 8, a * side : (a + 1) * side
+            ]
         for half in range(2):
             row = group * 8 + half * 4
             cells = jnp.concatenate(
                 [
-                    jnp.concatenate([back[row], back[row + 2]], axis=1),
-                    jnp.concatenate([back[row + 1], back[row + 3]], axis=1),
+                    jnp.concatenate([cells_by_row[row], cells_by_row[row + 2]], axis=1),
+                    jnp.concatenate([cells_by_row[row + 1], cells_by_row[row + 3]], axis=1),
                 ],
                 axis=0,
             )
@@ -483,13 +543,13 @@
             filt_r = jnp.concatenate([filter_real[...]] * 2, axis=0)
             filt_i = jnp.concatenate([filter_imag[...]] * 2, axis=0)
             done = inverse_of(real * filt_r - imag * filt_i, real * filt_i + imag * filt_r)
-            back[row] = done[:side, :side]
-            back[row + 1] = done[side:, :side]
-            back[row + 2] = done[:side, side:]
-            back[row + 3] = done[side:, side:]
+            cells_by_row[row] = done[:side, :side]
+            cells_by_row[row + 1] = done[side:, :side]
+            cells_by_row[row + 2] = done[:side, side:]
+            cells_by_row[row + 3] = done[side:, side:]
         for a in range(side):
             cut = slice(a * side, (a + 1) * side)
-            out[group * 8 : group * 8 + 8, cut] += flat_back[
+            out[group * 8 : group * 8 + 8, cut] += flat_cells[
                 pl.ds(group * 8 * side + a, 8, stride=side), :
             ]
 
@@ -498,10 +558,14 @@
 
     @pl.loop(1, count)
     def _(step):
-        tap_copy(step).wait_send()
-        px_copy(step).wait_send()
+        row_copy(step).wait_send()
+        col_copy(step).wait_send()
+        for piece in range(pieces):
+            px_copy(piece, step).wait_send()
+        for piece in range(last):
+            back_copy(piece, step).wait_send()
         for group in range(groups):
-            back_copy(group, step).wait_send()
+            last_copy(group, step).wait_send()
 
 
 def fits(pixels, row_taps, column_taps):
@@ -515,6 +579,7 @@
         and rows_dev % 16 == 0
         and 128 % rows_dev == 0
         and (count * rows_dev) % 128 == 0
+        and count % (128 // rows_dev) == 0
     )
 
 
@@ -527,51 +592,65 @@
     a_dev = cols_dev // 128
     groups = rows_dev // 8
     me = lax.axis_index("rows")
-    slots = -(-column_length // 1024) * 1024
-    wanted = (column_length - jnp.arange(slots, dtype=jnp.int32)) % column_length
-    wanted = jnp.where(jnp.arange(slots) < column_length, wanted, -1)
-    held = me * rows_dev + jnp.arange(rows_dev, dtype=jnp.int32)
+    pieces = 4
+    piece_cols = cols_dev // pieces
+    per_block = 128 // rows_dev
+    start = (per_block - 1 - me % per_block) * rows_dev
+    wanted = start + rows_dev - 1 - jnp.arange(128, dtype=jnp.int32)
+    held = jnp.arange(rows_dev, dtype=jnp.int32)
     placed = jnp.sum(
         jnp.where(wanted[:, None] == held[None, :], column_taps[None, :], 0.0), axis=1
-    )
-    taps = jnp.concatenate([row_taps.reshape(a_dev, 128), placed.reshape(slots // 128, 128)])
-    tables = [jnp.asarray(table) for table in host_tables(side)]
+    ).reshape(1, 128)
+    made = host_tables(side)
+    tables = jnp.asarray(np.stack(made[:4]))
+    twists = jnp.asarray(np.stack(made[4:]))
+    hbm = pl.BlockSpec(memory_space=pl.ANY)
     vmem = pl.BlockSpec(memory_space=pltpu.VMEM)
     f32, bf16 = jnp.float32, jnp.bfloat16
     dma = pltpu.SemaphoreType.DMA
     return pl.pallas_call(
-        functools.partial(kernel, (count, rows_dev, side)),
+        functools.partial(kernel, (count, rows_dev, side, pieces)),
         out_shape=jax.ShapeDtypeStruct(pixels.shape, f32),
-        in_specs=[vmem] * 4 + [pl.BlockSpec(memory_space=pltpu.SMEM)] + [vmem] * 6,
+        in_specs=[hbm, vmem, vmem, pl.BlockSpec(memory_space=pltpu.SMEM), hbm, hbm],
         out_specs=vmem,
         scratch_shapes=[
-            pltpu.VMEM((column_length, cols_dev), f32),
-            pltpu.VMEM((column_length, cols_dev), bf16),
-            pltpu.VMEM((column_length, cols_dev), bf16),
-            pltpu.VMEM((column_length, a_dev, 128), f32),
-            pltpu.VMEM((rows_dev, side, side), f32),
             pltpu.VMEM((rows_dev + 16, row_length), f32),
+            pltpu.VMEM(tables.shape, bf16),
+            pltpu.VMEM(twists.shape, f32),
             pltpu.VMEM((1, row_length), f32),
             pltpu.VMEM((1, row_length), f32),
-            pltpu.VMEM((count,) + taps.shape, f32),
+            pltpu.VMEM((pieces, column_length, piece_cols), f32),
+            pltpu.VMEM((pieces, column_length, piece_cols), bf16),
+            pltpu.VMEM((pieces, column_length, piece_cols), bf16),
+            pltpu.VMEM((pieces, column_length, piece_cols), f32),
+            pltpu.VMEM((rows_dev, row_length), f32),
+            pltpu.VMEM((rows_dev, side, side), f32),
+            pltpu.VMEM((1, row_length), f32),
+            pltpu.VMEM((1, row_length), f32),
+            pltpu.VMEM((count, a_dev, 128), f32),
+            pltpu.VMEM((count, 1, 128), f32),
             pltpu.VMEM((groups, count * 8, column_length), bf16),
             pltpu.VMEM((groups, count * 8, column_length), bf16),
             pltpu.VMEM((side, side), f32),
             pltpu.VMEM((side, side), f32),
+            dma((pieces, count)),
+            dma((pieces, count)),
             dma((count,)),
             dma((count,)),
             dma((count,)),
             dma((count,)),
             dma((2,)),
             dma((2,)),
+            dma((pieces, count)),
+            dma((pieces, count)),
             dma((groups, count)),
             dma((groups, count)),
-            dma((2 + groups,)),
+            dma((3,)),
         ],
         compiler_params=pltpu.CompilerParams(
-            collective_id=0, has_side_effects=True, vmem_limit_bytes=48 * 1024 * 1024
+            collective_id=0, has_side_effects=True, vmem_limit_bytes=60 * 1024 * 1024
         ),
-    )(pixels, pixels[:1], pixels[rows_dev - 1 :], taps, stencil, *tables)
+    )(pixels, row_taps.reshape(a_dev, 128), placed, stencil, tables, twists)
 
 
 def chosen(pixels, row_taps, column_taps, stencil):

time: 122 us -> 117 us (0.959)
  local copies, waits for them, and re-layouts: 10.2 us -> 3.05 us
  Pallas kernels: 110 us -> 113 us
    unnamed x17 -> x1, local copies, waits for them, and re-layouts: 8.88 us -> 3.05 us
    pallas_call x1, Pallas kernels: 110 us -> 113 us  [fused(): pl.pallas_call(functools.partial(kernel, (count, rows_dev, side, pieces))...]
    slice x1 -> x0, local copies, waits for them, and re-layouts: 1.29 us -> none  [fused(): pixels[rows_dev - 1:]]
where the time goes in v2:
time: 117 us
  Pallas kernels  113 us (97%)
  local copies, waits for them, and re-layouts  3.05 us (3%)
  other arithmetic  1.25 us (1%)
    pallas_call x1, Pallas kernels, fused(): pl.pallas_call(functools.partial(kernel, (count, rows_dev, side, pieces))...  113 us
    unnamed x1, local copies, waits for them, and re-layouts  3.05 us

profile of v2, /device:TPU:0, one launch (start us, length us, event | category | flops | bytes accessed | tf_op | source)
XLA Modules:
  0.0 117.2 jit_solution(5786745788472662998)
XLA Ops:
  0.0 1.3 %select_reduce_fusion = f32[128]{0:T(128)} fusion(f32[32]{0:T(128)} %param.8, s32[128]{0:T(128)S(1)} %iota_subtract_fusion), kind=kLoop, calls=%fused_computation | loop fusion | flops 12160 | bytes 1152 | tf_op jit(solution)/shard_map/reduce_sum | solution.py:601
  1.3 112.9 %shard_map.64 = f32[32,16384]{1,0:T(8,128)} custom-call(f32[32,16384]{1,0:T(8,128)} %pixels.1, f32[8,128]{1,0:T(8,128)} %bitcast.2, f32[1,128]{1,0:T(1,128)} %bitcast.3, f32[3,3]{1,0:T(4,128)} %stencil.1, bf16[4,256,256]{2,1,0:T(8,128)(2,1)} %constant.32.clone.tables_in, f32[2,128,128]{2,1,0:T(8,128)} %constant.33.clone.twists_in), custom_call_target="tpu_custom_call" | custom-call | tf_op jit(solution)/shard_map/pallas_call | solution.py:611
  114.2 3.0 %copy.8 = f32[32,16384]{1,0:T(8,128)} copy(f32[32,16384]{1,0:T(8,128)} %shard_map.64) | data formatting | bytes 4194304
  (1 shorter events, 0.0 us)

commit v3 on v2

--- a/solution.py
+++ b/solution.py
@@ -246,11 +246,29 @@
     own = slice(8, 8 + rows_dev)
     me = lax.axis_index("rows")
 
+    planes = count // 4
+    plane, core = me // 4, lax.rem(me, 2)
+    way = jnp.where(plane < planes // 2, 1, planes - 1)
+
+    def near(step):
+        return plane * 4 + lax.rem(me + step, 4)
+
+    def far(step):
+        hop, turn = step % (planes - 1) + 1, step // (planes - 1)
+        hop = lax.rem(hop + core * 1 - 1, planes - 1) + 1
+        return lax.rem(plane + way * hop, planes) * 4 + lax.rem(me + turn, 4)
+
+    def to_all(start):
+        @pl.loop(1, 4)
+        def _(step):
+            start(near(step))
+
+        @pl.loop(0, count - 4)
+        def _(step):
+            start(far(step))
+
     def peer(step):
         return lax.rem(me + step, count)
-
-    def source(step):
-        return lax.rem(me + count - step, count)
 
     load_px = pltpu.make_async_copy(pixels, padded.at[own, :], local_sem.at[0])
     load_tables = pltpu.make_async_copy(tables_in, tables, local_sem.at[1])
@@ -273,32 +291,31 @@
     def rows_of(rank):
         return pl.ds(pl.multiple_of(rank * rows_dev, 16), rows_dev)
 
-    def px_copy(piece, step):
-        to = peer(step)
+    def px_copy(piece, to, source):
         return pltpu.make_async_remote_copy(
             src_ref=padded.at[own, columns_of(to, piece)],
             dst_ref=recv.at[piece, rows_of(me), :],
-            send_sem=send_px.at[piece, step],
-            recv_sem=recv_px.at[piece, step],
+            send_sem=send_px.at[piece, to],
+            recv_sem=recv_px.at[piece, source],
             device_id={"rows": to},
         )
 
-    def row_copy(step):
+    def row_copy(to, source):
         return pltpu.make_async_remote_copy(
             src_ref=row_taps,
             dst_ref=all_row.at[me],
-            send_sem=send_row.at[step],
-            recv_sem=recv_row.at[step],
-            device_id={"rows": peer(step)},
-        )
-
-    def col_copy(step):
+            send_sem=send_row.at[to],
+            recv_sem=recv_row.at[source],
+            device_id={"rows": to},
+        )
+
+    def col_copy(to, source):
         return pltpu.make_async_remote_copy(
             src_ref=column_taps,
             dst_ref=all_column.at[me],
-            send_sem=send_col.at[step],
-            recv_sem=recv_col.at[step],
-            device_id={"rows": peer(step)},
+            send_sem=send_col.at[to],
+            recv_sem=recv_col.at[source],
+            device_id={"rows": to},
         )
 
     def halo_copy(which):
@@ -312,25 +329,21 @@
 
     load_px.wait()
 
-    @pl.loop(1, count)
-    def _(step):
-        px_copy(0, step).start()
-        col_copy(step).start()
+    def first_out(to):
+        px_copy(0, to, me).start()
+        col_copy(to, me).start()
+
+    to_all(first_out)
 
     top_row[...] = padded[8:9, :]
     bottom_row[...] = padded[7 + rows_dev : 8 + rows_dev, :]
     halo_copy(0).start()
     halo_copy(1).start()
 
-    @pl.loop(1, count)
-    def _(step):
-        row_copy(step).start()
+    to_all(lambda to: row_copy(to, me).start())
 
     for piece in range(1, pieces):
-
-        @pl.loop(1, count)
-        def _(step, piece=piece):
-            px_copy(piece, step).start()
+        to_all(lambda to, piece=piece: px_copy(piece, to, me).start())
 
     all_row[me] = row_taps[...]
     all_column[me] = column_taps[...]
@@ -339,7 +352,7 @@
 
     @pl.loop(1, count)
     def _(step):
-        col_copy(step).wait_recv()
+        col_copy(peer(step), peer(step)).wait_recv()
 
     per_block = 128 // rows_dev
     lines = []
@@ -412,7 +425,7 @@
     def filter_spectrum():
         @pl.loop(1, count)
         def _(step):
-            row_copy(step).wait_recv()
+            row_copy(peer(step), peer(step)).wait_recv()
 
         row_filter = jnp.concatenate([all_row[rank] for rank in range(count)], axis=0)
         nothing = jnp.zeros_like(row_filter)
@@ -447,25 +460,23 @@
                 sums[1] + pltpu.roll(sums[0], 1, 1) + pltpu.roll(sums[2], width - 1, 1)
             )
 
-    def back_copy(piece, step):
-        to = peer(step)
+    def back_copy(piece, to, source):
         return pltpu.make_async_remote_copy(
             src_ref=ready.at[piece, rows_of(to), :],
             dst_ref=back.at[:, columns_of(me, piece)],
-            send_sem=send_back.at[piece, step],
-            recv_sem=recv_back.at[piece, step],
+            send_sem=send_back.at[piece, to],
+            recv_sem=recv_back.at[piece, source],
             device_id={"rows": to},
         )
 
     last = pieces - 1
 
-    def last_copy(group, step):
-        to = peer(step)
+    def last_copy(group, to, source):
         return pltpu.make_async_remote_copy(
             src_ref=ready.at[last, pl.ds(pl.multiple_of(to * rows_dev + group * 8, 8), 8), :],
             dst_ref=back.at[pl.ds(group * 8, 8), columns_of(me, last)],
-            send_sem=send_last.at[group, step],
-            recv_sem=recv_last.at[group, step],
+            send_sem=send_last.at[group, to],
+            recv_sem=recv_last.at[group, source],
             device_id={"rows": to},
         )
 
@@ -487,8 +498,9 @@
 
         @pl.loop(1, count)
         def _(step, piece=piece):
-            px_copy(piece, step).wait_recv()
-            take(piece, source(step), recv[piece, rows_of(source(step)), :])
+            source = peer(step)
+            px_copy(piece, source, source).wait_recv()
+            take(piece, source, recv[piece, rows_of(source), :])
 
         for group in range(groups):
             done = filtered_rows(piece, group)
@@ -496,16 +508,10 @@
                 at = rank * rows_dev + group * 8
                 ready[piece, at : at + 8, :] = done[rank * 8 : rank * 8 + 8]
             if piece == last:
-
-                @pl.loop(1, count)
-                def _(step, group=group):
-                    last_copy(group, step).start()
+                to_all(lambda to, group=group: last_copy(group, to, me).start())
 
         if piece != last:
-
-            @pl.loop(1, count)
-            def _(step, piece=piece):
-                back_copy(piece, step).start()
+            to_all(lambda to, piece=piece: back_copy(piece, to, me).start())
 
         back[:, columns_of(me, piece)] = ready[piece, rows_of(me), :]
         if piece == 0:
@@ -517,13 +523,13 @@
 
         @pl.loop(1, count)
         def _(step, piece=piece):
-            back_copy(piece, step).wait_recv()
+            back_copy(piece, peer(step), peer(step)).wait_recv()
 
     for group in range(groups):
 
         @pl.loop(1, count)
         def _(step, group=group):
-            last_copy(group, step).wait_recv()
+            last_copy(group, peer(step), peer(step)).wait_recv()
 
         for a in range(side):
             flat_cells[pl.ds(group * 8 * side + a, 8, stride=side), :] = back[
@@ -558,14 +564,14 @@
 
     @pl.loop(1, count)
     def _(step):
-        row_copy(step).wait_send()
-        col_copy(step).wait_send()
+        row_copy(peer(step), peer(step)).wait_send()
+        col_copy(peer(step), peer(step)).wait_send()
         for piece in range(pieces):
-            px_copy(piece, step).wait_send()
+            px_copy(piece, peer(step), peer(step)).wait_send()
         for piece in range(last):
-            back_copy(piece, step).wait_send()
+            back_copy(piece, peer(step), peer(step)).wait_send()
         for group in range(groups):
-            last_copy(group, step).wait_send()
+            last_copy(group, peer(step), peer(step)).wait_send()
 
 
 def fits(pixels, row_taps, column_taps):
@@ -580,6 +586,8 @@
         and 128 % rows_dev == 0
         and (count * rows_dev) % 128 == 0
         and count % (128 // rows_dev) == 0
+        and count % 4 == 0
+        and count > 8
     )
 
 
@@ -592,7 +600,7 @@
     a_dev = cols_dev // 128
     groups = rows_dev // 8
     me = lax.axis_index("rows")
-    pieces = 4
+    pieces = 2
     piece_cols = cols_dev // pieces
     per_block = 128 // rows_dev
     start = (per_block - 1 - me % per_block) * rows_dev

time: 117 us -> 113 us (0.966)
  Pallas kernels: 113 us -> 108 us
    pallas_call x1, Pallas kernels: 113 us -> 108 us  [fused(): pl.pallas_call(functools.partial(kernel, (count, rows_dev, side, pieces))...]
where the time goes in v3:
time: 113 us; the launch traced here: 112 us
  Pallas kernels  108 us (96%)
  local copies, waits for them, and re-layouts  3.05 us (3%)
  other arithmetic  1.25 us (1%)
    pallas_call x1, Pallas kernels, fused(): pl.pallas_call(functools.partial(kernel, (count, rows_dev, side, pieces))...  108 us
    unnamed x1, local copies, waits for them, and re-layouts  3.05 us

profile of v3, /device:TPU:0, one launch (start us, length us, event | category | flops | bytes accessed | tf_op | source)
XLA Modules:
  0.0 112.3 jit_solution(5031145912430732451)
XLA Ops:
  0.0 1.3 %select_reduce_fusion = f32[128]{0:T(128)} fusion(f32[32]{0:T(128)} %param.8, s32[128]{0:T(128)S(1)} %iota_subtract_fusion), kind=kLoop, calls=%fused_computation | loop fusion | flops 12160 | bytes 1152 | tf_op jit(solution)/shard_map/reduce_sum | solution.py:609
  1.3 107.9 %shard_map.64 = f32[32,16384]{1,0:T(8,128)} custom-call(f32[32,16384]{1,0:T(8,128)} %pixels.1, f32[8,128]{1,0:T(8,128)} %bitcast.2, f32[1,128]{1,0:T(1,128)} %bitcast.3, f32[3,3]{1,0:T(4,128)} %stencil.1, bf16[4,256,256]{2,1,0:T(8,128)(2,1)} %constant.32.clone.tables_in, f32[2,128,128]{2,1,0:T(8,128)} %constant.33.clone.twists_in), custom_call_target="tpu_custom_call" | custom-call | tf_op jit(solution)/shard_map/pallas_call | solution.py:619
  109.2 3.0 %copy.8 = f32[32,16384]{1,0:T(8,128)} copy(f32[32,16384]{1,0:T(8,128)} %shard_map.64) | data formatting | bytes 4194304
  (1 shorter events, 0.0 us)
